TPU v7x, 512 devices: a whole 4x4x16 slice. The times are simulated.
512 devices in a mesh: rows: 32 (over x_lo, z), ka: 16 (over x_hi, y, core).
Axes of the slice: x: 4 (x_hi: 2, x_lo: 2; x = x_hi * 2 + x_lo), y: 4, z: 16, core: 2. Of those that a mesh axis runs over, the one named last changes fastest.
Arguments:
- pair_repr: bfloat16 [512, 512, 128], P('rows', 'ka'), may hold values from -6 to 6
- pair_mask: int32 [512, 512], P('rows', 'ka'), may hold values 0 or 1
- ln_gain: float32 [128], replicated, may hold values from 0.1 to 1.9
- ln_bias: float32 [128], replicated, may hold values from -3 to 3
- w_proj: bfloat16 [128, 256], replicated, may hold values from -0.5 to 0.5
- w_gate: bfloat16 [128, 256], replicated, may hold values from -0.5 to 0.5
- w_out_gate: bfloat16 [128, 128], replicated, may hold values from -0.5 to 0.5
- out_gain: float32 [128], replicated, may hold values from 0.1 to 1.9
- out_bias: float32 [128], replicated, may hold values from -3 to 3
- w_out: bfloat16 [128, 128], replicated, may hold values from -0.5 to 0.5
Outputs:
- update: bfloat16 [512, 512, 128], P('rows', 'ka')
All inputs are finite; a program needn't handle non-finite values. No bound on the sum of `pair_mask` on one device may be relied on, other than what follows from the above.
Results may differ from a plain program's by a relative error of at most 0.015.
Values may be sent and summed in bfloat16 or wider, within the bound.
A program may use at most 64 MiB of HBM per device.

v0:
```python
import jax
import jax.numpy as jnp
from jax import lax
from jax.sharding import Mesh
from jax.sharding import PartitionSpec as P

ROWS = ("rows_0", "rows_1")
KA = ("ka_0", "ka_1", "ka_2")


def joined_along(blocks, dim):
    blocks = jnp.moveaxis(blocks, 0, dim)
    dims = blocks.shape
    return blocks.reshape(*dims[:dim], dims[dim] * dims[dim + 1], *dims[dim + 2 :])


def stacked_from(array, axes, order):
    blocks = array[None]
    for k in order:
        blocks = lax.all_gather(blocks, axes[k], axis=0, tiled=True)
    carried = [lax.axis_size(axes[k]) for k in reversed(order)]
    blocks = blocks.reshape(*carried, *array.shape)
    turned = sorted(range(len(order)), key=lambda place: order[len(order) - 1 - place])
    return blocks.transpose(*turned, *range(len(order), blocks.ndim)).reshape(-1, *array.shape)


def whole_of(array, axes, order, dim):
    return joined_along(stacked_from(array, axes, order), dim)


def split_up(array, dim, count):
    dims = array.shape
    blocks = array.reshape(*dims[:dim], count, dims[dim] // count, *dims[dim + 1 :])
    return jnp.moveaxis(blocks, dim, 0)


def sum_at_owner(array, axis, dim):
    blocks = split_up(array, dim, lax.axis_size(axis))
    arrived = lax.all_to_all(blocks, axis, split_axis=0, concat_axis=0, tiled=True)
    return arrived.astype(jnp.float32).sum(axis=0)


def sum_in_two_steps(array, axes, dim):
    far, near = axes
    blocks = split_up(array, dim, lax.axis_size(far))
    nearer = sum_at_owner(blocks, near, dim + 1)
    arrived = lax.all_to_all(
        nearer.astype(jnp.bfloat16), far, split_axis=0, concat_axis=0, tiled=True
    )
    return arrived.astype(jnp.float32).sum(axis=0)


def layer_norm(values, gain_vec, bias_vec):
    center = jnp.mean(values, axis=-1, keepdims=True)
    deviate = values - center
    spread = jnp.mean(deviate * deviate, axis=-1, keepdims=True)
    return deviate * lax.rsqrt(spread + 1e-05) * gain_vec + bias_vec


def panel_sums(left_edge, right_edge):
    return jnp.einsum(
        "ikh,jkh->ijh",
        left_edge,
        whole_of(right_edge, ROWS, (0, 1), 0),
        preferred_element_type=jnp.float32,
    )


def body(
    pair_repr, pair_mask, ln_gain, ln_bias, w_proj, w_gate, w_out_gate, out_gain, out_bias, w_out
):
    row_count, col_count, chans = pair_repr.shape
    hidden = w_out.shape[0]
    normed = layer_norm(pair_repr.astype(jnp.float32), ln_gain, ln_bias).astype(jnp.bfloat16)
    flat_rows = normed.reshape(row_count * col_count, chans)
    projected = jnp.dot(flat_rows, w_proj, preferred_element_type=jnp.float32)
    gate_logits = jnp.dot(flat_rows, w_gate, preferred_element_type=jnp.float32)
    mask_col = pair_mask.reshape(row_count * col_count, 1).astype(jnp.float32)
    edges = (jax.nn.sigmoid(gate_logits) * projected * mask_col).astype(jnp.bfloat16)
    edges = edges.reshape(row_count, col_count, 2 * hidden)
    left_edge = edges[:, :, :hidden]
    right_edge = edges[:, :, hidden:]
    partial_sums = panel_sums(left_edge, right_edge)
    triangle = sum_in_two_steps(partial_sums.astype(jnp.bfloat16), (("ka_0", "ka_1"), "ka_2"), 1)
    tri_normed = layer_norm(triangle, out_gain, out_bias).astype(jnp.bfloat16)
    out_gate = jax.nn.sigmoid(jnp.dot(flat_rows, w_out_gate, preferred_element_type=jnp.float32))
    projected_out = jnp.dot(
        tri_normed.reshape(row_count * col_count, hidden), w_out, preferred_element_type=jnp.float32
    )
    return (out_gate * projected_out).astype(jnp.bfloat16).reshape(row_count, col_count, chans)


def solution(mesh):
    torus = Mesh(mesh.devices.reshape(2, 16, 2, 4, 2), ("rows_0", "rows_1", "ka_0", "ka_1", "ka_2"))
    placed = (P(ROWS, KA, None), P(ROWS, KA), P(), P(), P(), P(), P(), P(), P(), P())
    return jax.shard_map(
        body, mesh=torus, in_specs=placed, out_specs=P(ROWS, KA, None), check_vma=False
    )
```

profile of v0, /device:TPU:32, one launch (start us, length us, event | category | flops | bytes accessed | tf_op | source)
XLA Modules:
  0.0 160.8 jit_solution(4884521978984217984)
XLA Ops:
  6.5 0.0 copy-start
  6.5 0.0 all-gather.3.cloned.1.call-start
  6.5 1.1 convert_reduce_fusion.2
  7.6 1.2 fusion.11
  8.8 0.7 convert_element_type.40
  9.5 0.1 convert_element_type.41
  9.6 1.1 fusion.14
  10.7 0.0 copy-done
  10.7 0.3 fusion.2
  11.0 1.1 fusion.4
  12.2 6.0 %all-gather = bf16[32,32,128]{2,1,0:T(8,128)(2,1)} all-gather(bf16[16,32,128]{2,1,0:T(8,128)(2,1)S(1)} %get-tuple-element.7), channel_id=2, replica_groups=mesh['rows_0'=2,'rows_1'=16,'ka_0'=2,'ka_1'=4,'ka_2'=2] {'rows_0'}, dimensions={0}, use_global_device_ids=true | all-gather | bytes 393216 | tf_op jit(solution)/shard_map/all_gather | solution.py:20
  18.2 0.0 all-gather.3.cloned.1.call-update
  18.2 0.4 copy.30
  18.6 81.8 %all-gather.3.cloned.1.call-done = bf16[32,16,32,128]{3,2,1,0:T(8,128)(2,1)} async-done(((bf16[2,16,32,128]{3,2,1,0:T(8,128)(2,1)}), bf16[32,16,32,128]{3,2,1,0:T(8,128)(2,1)}) %all-gather.3.cloned.1.call-update) | async-done | bytes 4194320 | tf_op jit(solution)/shard_map/all_gather | solution.py:20
  100.4 5.3 %copy.23 = bf16[2,16,16,32,128]{4,3,2,1,0:T(8,128)(2,1)} copy(bf16[2,16,16,32,128]{4,3,2,0,1:T(8,128)(2,1)} %bitcast.39) | data formatting | bytes 8388608 | tf_op jit(solution)/shard_map/transpose | solution.py:24
  105.8 8.6 %copy.25 = bf16[512,32,128]{0,1,2:T(8,128)(2,1)} copy(bf16[512,32,128]{2,1,0:T(8,128)(2,1)} %bitcast.37) | data formatting | bytes 8388608 | tf_op jit(solution)/shard_map/reshape;reshape | solution.py:14
  114.4 2.9 %convert_bitcast_fusion = bf16[16,512,128]{1,0,2:T(8,128)(2,1)S(1)} fusion(bf16[16,32,128]{1,0,2:T(8,128)(2,1)S(1)} %copy.30, bf16[512,32,128]{0,1,2:T(8,128)(2,1)} %copy.25), kind=kOutput, calls=%fused_computation.2 | convolution fusion | flops 68157440 | bytes 6422528 | tf_op jit(solution)/shard_map/ikh,jkh->ijh/dot_general | solution.py:61
  117.3 3.1 %copy.26 = bf16[16,512,128]{2,1,0:T(8,128)(2,1)} copy(bf16[16,512,128]{1,0,2:T(8,128)(2,1)S(1)} %convert_bitcast_fusion) | data formatting | bytes 4194304 | tf_op jit(solution)/shard_map/convert_element_type | solution.py:84
  120.4 2.1 %copy.28 = bf16[2,8,16,32,128]{4,3,2,1,0:T(8,128)(2,1)S(1)} copy(bf16[2,8,16,32,128]{4,3,0,1,2:T(8,128)(2,1)} %bitcast.38) | data formatting | bytes 4194304 | tf_op jit(solution)/shard_map/transpose | solution.py:34
  122.5 0.0 copy-start.4
  122.5 5.4 %all_to_all.10 = bf16[2,8,16,32,128]{4,3,2,1,0:T(8,128)(2,1)S(1)} all-to-all(bf16[2,8,16,32,128]{4,3,2,1,0:T(8,128)(2,1)S(1)} %copy.28), channel_id=1, replica_groups=mesh['rows_0'=2,'rows_1'=16,'ka_0'=2,'ka_1'=4,'ka_2'=2] {'ka_2'}, dimensions={0} | all-to-all | bytes 4194304 | tf_op jit(solution)/shard_map/all_to_all | solution.py:39
  128.0 0.0 copy-start.2
  128.0 0.0 copy-start.3
  128.0 0.0 copy-start.1
  128.0 1.7 %reduce_sum.61 = bf16[8,16,32,128]{3,2,1,0:T(8,128)(2,1)} reduce(bf16[2,8,16,32,128]{4,3,2,1,0:T(8,128)(2,1)S(1)} %all_to_all.10, bf16[]{:T(256)} %constant.14.clone.1), dimensions={0}, to_apply=%region_2.0 | reduce | flops 524288 | bytes 3145730 | tf_op jit(solution)/shard_map/reduce_sum | solution.py:40
  129.7 6.7 %all-to-all-start.1 = ((bf16[8,16,32,128]{3,2,1,0:T(8,128)(2,1)}), bf16[8,16,32,128]{3,2,1,0:T(8,128)(2,1)S(1)}, u32[]{:S(2)}, u32[]{:S(2)}) async-start(bf16[8,16,32,128]{3,2,1,0:T(8,128)(2,1)} %reduce_sum.61), calls=%async_computation.1 | async-start | bytes 2097152 | tf_op jit(solution)/shard_map/all_to_all | solution.py:47
  136.4 0.0 copy-done.4
  136.4 0.2 fusion.7
  136.6 15.6 %all-to-all-done.1 = bf16[8,16,32,128]{3,2,1,0:T(8,128)(2,1)S(1)} async-done(((bf16[8,16,32,128]{3,2,1,0:T(8,128)(2,1)}), bf16[8,16,32,128]{3,2,1,0:T(8,128)(2,1)S(1)}, u32[]{:S(2)}, u32[]{:S(2)}) %all-to-all-start.1) | async-done | bytes 1048608 | tf_op jit(solution)/shard_map/all_to_all | solution.py:47
  152.2 0.2 convert_reduce_fusion
  152.4 0.1 div.25
  152.5 0.3 multiply_reduce_fusion
  152.8 0.1 rsqrt.21
  152.9 0.0 copy-done.2
  152.9 0.0 copy-done.3
  152.9 0.2 fusion.18
  153.1 0.0 copy-done.1
  153.1 0.8 fusion.8
  (5 shorter events, 0.1 us)
Async XLA Ops:
  6.5 4.2 %copy-start = (bf16[128,256]{1,0:T(8,128)(2,1)S(1)}, bf16[128,256]{1,0:T(8,128)(2,1)}, u32[]{:S(2)}) copy-start(bf16[128,256]{1,0:T(8,128)(2,1)} %param.15) | copy-start | bytes 196612
  6.5 93.9 %all-gather.3.cloned.1.call-start = ((), (), s32[]{:S(2)}) async-start(), calls=%async_computation.2 | async-start | bytes 4456448 | tf_op jit(solution)/shard_map/all_gather | solution.py:20
  122.5 13.8 %copy-start.4 = (bf16[128,128]{1,0:T(8,128)(2,1)S(1)}, bf16[128,128]{1,0:T(8,128)(2,1)}, u32[]{:S(2)}) copy-start(bf16[128,128]{1,0:T(8,128)(2,1)} %param.16) | copy-start | bytes 98308
  128.0 24.9 %copy-start.2 = (f32[128]{0:T(128)S(1)}, f32[128]{0:T(128)}, u32[]{:S(2)}) copy-start(f32[128]{0:T(128)} %param.18) | copy-start | bytes 1540
  128.0 24.9 %copy-start.3 = (f32[128]{0:T(128)S(1)}, f32[128]{0:T(128)}, u32[]{:S(2)}) copy-start(f32[128]{0:T(128)} %param.17) | copy-start | bytes 1540
  128.0 25.1 %copy-start.1 = (bf16[128,128]{1,0:T(8,128)(2,1)S(1)}, bf16[128,128]{1,0:T(8,128)(2,1)}, u32[]{:S(2)}) copy-start(bf16[128,128]{1,0:T(8,128)(2,1)} %param.19) | copy-start | bytes 98308
  129.7 22.6 %all-to-all-start.1 = ((bf16[8,16,32,128]{3,2,1,0:T(8,128)(2,1)}), bf16[8,16,32,128]{3,2,1,0:T(8,128)(2,1)S(1)}, u32[]{:S(2)}, u32[]{:S(2)}) async-start(bf16[8,16,32,128]{3,2,1,0:T(8,128)(2,1)} %reduce_sum.61), calls=%async_computation.1 | async-start | bytes 2097152 | tf_op jit(solution)/shard_map/all_to_all | solution.py:47
Sparse Core Ops, SparseCore 0:
  18.3 82.0 all-gather.2
where the time goes:
time: 161 us
  waiting for transfers between devices  97.5 us (61%)
  local copies, waits for them, and re-layouts  20 us (12%)
  between operations  13.6 us (8%)
  blocking collectives  11.4 us (7%)
  starting transfers between devices  6.71 us (4%)
  other arithmetic  6.43 us (4%)
  matrix products  5.26 us (3%)
    all_gather x1, waiting for transfers between devices, stacked_from(): blocks = lax.all_gather(blocks, axes[k], axis=0, tiled=True)  81.8 us
    all_to_all x1, waiting for transfers between devices, sum_in_two_steps(): lax.all_to_all(nearer.astype(jnp.bfloat16), far, split_axis=0, concat_axi...  15.6 us
    another operation x1, local copies, waits for them, and re-layouts, joined_along(): blocks.reshape(*dims[:dim], dims[dim] * dims[dim + 1], *dims[dim + 2:])  8.64 us
    all_to_all x1, starting transfers between devices, sum_in_two_steps(): lax.all_to_all(nearer.astype(jnp.bfloat16), far, split_axis=0, concat_axi...  6.71 us
    all_gather x1, blocking collectives, stacked_from(): blocks = lax.all_gather(blocks, axes[k], axis=0, tiled=True)  6 us
    all_to_all x1, blocking collectives, sum_at_owner(): lax.all_to_all(blocks, axis, split_axis=0, concat_axis=0, tiled=True)  5.42 us
    transpose x1, local copies, waits for them, and re-layouts, stacked_from(): blocks.transpose(*turned, *range(len(order), blocks.ndim))  5.33 us
  transfers between devices with their start and end apart: 2, of which 2 were waited for; matrix products, arithmetic and copies ran while one was open for 0% of the time, Pallas kernels for 0%

commit v1 on v0

--- a/solution.py
+++ b/solution.py
@@ -17,7 +17,9 @@
 def stacked_from(array, axes, order):
     blocks = array[None]
     for k in order:
-        blocks = lax.all_gather(blocks, axes[k], axis=0, tiled=True)
+        blocks = jnp.concatenate(
+            lax.all_to_all(jnp.stack([blocks] * lax.axis_size(axes[k])), axes[k], 0, 0), axis=0
+        )
     carried = [lax.axis_size(axes[k]) for k in reversed(order)]
     blocks = blocks.reshape(*carried, *array.shape)
     turned = sorted(range(len(order)), key=lambda place: order[len(order) - 1 - place])

time: 161 us -> 268 us (1.66)
  waiting for transfers between devices: 97.5 us -> 197 us
  starting transfers between devices: 6.71 us -> 22.3 us
  between operations: 13.6 us -> 0.17 us
  local copies, waits for them, and re-layouts: 20 us -> 22.9 us
    all_to_all x0 -> x1, waiting for transfers between devices: none -> 182 us  [stacked_from(): lax.all_to_all(jnp.stack([blocks] * lax.axis_size(axes[k])), axes[k], 0, 0)]
    all_gather x1 -> x0, waiting for transfers between devices: 81.8 us -> none  [stacked_from(): blocks = lax.all_gather(blocks, axes[k], axis=0, tiled=True)]
    all_to_all x0 -> x1, starting transfers between devices: none -> 15.2 us  [stacked_from(): lax.all_to_all(jnp.stack([blocks] * lax.axis_size(axes[k])), axes[k], 0, 0)]
    all_to_all x0 -> x1, blocking collectives: none -> 7.83 us  [stacked_from(): lax.all_to_all(jnp.stack([blocks] * lax.axis_size(axes[k])), axes[k], 0, 0)]
    all_gather x1 -> x0, blocking collectives: 6 us -> none  [stacked_from(): blocks = lax.all_gather(blocks, axes[k], axis=0, tiled=True)]
    all_to_all x0 -> x1, local copies, waits for them, and re-layouts: none -> 5.33 us  [stacked_from(): lax.all_to_all(jnp.stack([blocks] * lax.axis_size(axes[k])), axes[k], 0, 0)]
    transpose x1 -> x0, local copies, waits for them, and re-layouts: 5.33 us -> none  [stacked_from(): blocks.transpose(*turned, *range(len(order), blocks.ndim))]
    another operation x0 -> x2, local copies, waits for them, and re-layouts: none -> 2.96 us  [stacked_from(): jnp.stack([blocks] * lax.axis_size(axes[k]))]
where the time goes in v1:
time: 268 us
  waiting for transfers between devices  197 us (74%)
  local copies, waits for them, and re-layouts  22.9 us (9%)
  starting transfers between devices  22.3 us (8%)
  blocking collectives  13.3 us (5%)
  other arithmetic  6.45 us (2%)
  matrix products  5.26 us (2%)
    all_to_all x1, waiting for transfers between devices, stacked_from(): lax.all_to_all(jnp.stack([blocks] * lax.axis_size(axes[k])), axes[k], 0, 0)  182 us
    all_to_all x1, waiting for transfers between devices, sum_in_two_steps(): lax.all_to_all(nearer.astype(jnp.bfloat16), far, split_axis=0, concat_axi...  15.6 us
    all_to_all x1, starting transfers between devices, stacked_from(): lax.all_to_all(jnp.stack([blocks] * lax.axis_size(axes[k])), axes[k], 0, 0)  15.2 us
    another operation x1, local copies, waits for them, and re-layouts, joined_along(): blocks.reshape(*dims[:dim], dims[dim] * dims[dim + 1], *dims[dim + 2:])  8.64 us
    all_to_all x1, blocking collectives, stacked_from(): lax.all_to_all(jnp.stack([blocks] * lax.axis_size(axes[k])), axes[k], 0, 0)  7.83 us
    all_to_all x1, starting transfers between devices, sum_in_two_steps(): lax.all_to_all(nearer.astype(jnp.bfloat16), far, split_axis=0, concat_axi...  7.11 us
    all_to_all x1, blocking collectives, sum_at_owner(): lax.all_to_all(blocks, axis, split_axis=0, concat_axis=0, tiled=True)  5.42 us
  transfers between devices with their start and end apart: 2, of which 2 were waited for; matrix products, arithmetic and copies ran while one was open for 0% of the time, Pallas kernels for 0%

profile of v1, /device:TPU:32, one launch (start us, length us, event | category | flops | bytes accessed | tf_op | source)
XLA Modules:
  0.0 267.5 jit_solution(10425348278724128670)
XLA Ops:
  0.0 0.0 copy-start
  0.0 1.1 convert_reduce_fusion.2
  1.1 1.2 fusion.11
  2.3 0.7 convert_element_type.40
  3.0 0.1 convert_element_type.41
  3.1 1.1 fusion.14
  4.2 0.0 copy-done
  4.2 0.3 fusion.2
  4.5 1.1 fusion.4
  5.6 7.8 %all_to_all.20 = bf16[2,1,16,32,128]{4,3,2,1,0:T(8,128)(2,1)S(1)} all-to-all(bf16[2,1,16,32,128]{4,3,2,1,0:T(8,128)(2,1)S(1)} %pad_maximum_fusion), channel_id=1, replica_groups=mesh['rows_0'=2,'rows_1'=16,'ka_0'=2,'ka_1'=4,'ka_2'=2] {'rows_0'}, dimensions={0} | all-to-all | bytes 524288 | tf_op jit(solution)/shard_map/all_to_all | solution.py:21
  13.5 2.9 %stack.7 = bf16[16,2,16,32,128]{4,3,2,1,0:T(8,128)(2,1)} broadcast(bf16[2,16,32,128]{3,2,1,0:T(8,128)(2,1)S(1)} %bitcast.40), dimensions={1,2,3,4} | broadcast | bytes 4456448 | tf_op jit(solution)/shard_map/stack | solution.py:21
  16.4 15.2 %all-to-all-start.1 = ((bf16[16,2,16,32,128]{4,3,2,1,0:T(8,128)(2,1)}), bf16[16,2,16,32,128]{4,3,2,1,0:T(8,128)(2,1)}, u32[]{:S(2)}, u32[]{:S(2)}) async-start(bf16[16,2,16,32,128]{4,3,2,1,0:T(8,128)(2,1)} %stack.7), calls=%async_computation.1 | async-start | bytes 8388608 | tf_op jit(solution)/shard_map/all_to_all | solution.py:21
  31.6 0.4 copy.30
  32.0 181.6 %all-to-all-done.1 = bf16[16,2,16,32,128]{4,3,2,1,0:T(8,128)(2,1)} async-done(((bf16[16,2,16,32,128]{4,3,2,1,0:T(8,128)(2,1)}), bf16[16,2,16,32,128]{4,3,2,1,0:T(8,128)(2,1)}, u32[]{:S(2)}, u32[]{:S(2)}) %all-to-all-start.1) | async-done | bytes 4194336 | tf_op jit(solution)/shard_map/all_to_all | solution.py:21
  213.6 5.3 %copy.23 = bf16[16,2,16,32,128]{4,3,2,0,1:T(8,128)(2,1)} copy(bf16[16,2,16,32,128]{4,3,2,1,0:T(8,128)(2,1)} %all-to-all-done.1) | data formatting | bytes 8388608 | tf_op jit(solution)/shard_map/all_to_all | solution.py:21
  218.9 8.6 %copy.25 = bf16[512,32,128]{0,1,2:T(8,128)(2,1)} copy(bf16[512,32,128]{2,1,0:T(8,128)(2,1)} %bitcast.38) | data formatting | bytes 8388608 | tf_op jit(solution)/shard_map/reshape;reshape | solution.py:14
  227.6 2.9 %convert_bitcast_fusion = bf16[16,512,128]{1,0,2:T(8,128)(2,1)S(1)} fusion(bf16[16,32,128]{1,0,2:T(8,128)(2,1)S(1)} %copy.30, bf16[512,32,128]{0,1,2:T(8,128)(2,1)} %copy.25), kind=kOutput, calls=%fused_computation.2 | convolution fusion | flops 68157440 | bytes 6422528 | tf_op jit(solution)/shard_map/ikh,jkh->ijh/dot_general | solution.py:63
  230.5 3.1 %copy.26 = bf16[16,512,128]{2,1,0:T(8,128)(2,1)} copy(bf16[16,512,128]{1,0,2:T(8,128)(2,1)S(1)} %convert_bitcast_fusion) | data formatting | bytes 4194304 | tf_op jit(solution)/shard_map/convert_element_type | solution.py:86
  233.6 2.1 copy.28
  235.7 0.0 copy-start.4
  235.7 5.4 %all_to_all.21 = bf16[2,8,16,32,128]{4,3,2,1,0:T(8,128)(2,1)S(1)} all-to-all(bf16[2,8,16,32,128]{4,3,2,1,0:T(8,128)(2,1)S(1)} %copy.28), channel_id=1, replica_groups=mesh['rows_0'=2,'rows_1'=16,'ka_0'=2,'ka_1'=4,'ka_2'=2] {'ka_2'}, dimensions={0} | all-to-all | bytes 4194304 | tf_op jit(solution)/shard_map/all_to_all | solution.py:41
  241.2 0.0 copy-start.2
  241.2 0.0 copy-start.3
  241.2 0.0 copy-start.1
  241.2 1.7 reduce_sum.61
  242.8 7.1 %all-to-all-start.3 = ((bf16[8,16,32,128]{3,2,1,0:T(8,128)(2,1)}), bf16[8,16,32,128]{3,2,1,0:T(8,128)(2,1)S(1)}, u32[]{:S(2)}, u32[]{:S(2)}) async-start(bf16[8,16,32,128]{3,2,1,0:T(8,128)(2,1)} %reduce_sum.61), calls=%async_computation.3 | async-start | bytes 2097152 | tf_op jit(solution)/shard_map/all_to_all | solution.py:49
  250.0 0.0 copy-done.4
  250.0 0.2 fusion.7
  250.2 15.6 %all-to-all-done.3 = bf16[8,16,32,128]{3,2,1,0:T(8,128)(2,1)S(1)} async-done(((bf16[8,16,32,128]{3,2,1,0:T(8,128)(2,1)}), bf16[8,16,32,128]{3,2,1,0:T(8,128)(2,1)S(1)}, u32[]{:S(2)}, u32[]{:S(2)}) %all-to-all-start.3) | async-done | bytes 1048608 | tf_op jit(solution)/shard_map/all_to_all | solution.py:49
  265.8 0.2 convert_reduce_fusion
  266.0 0.1 div.25
  266.1 0.3 multiply_reduce_fusion
  266.4 0.1 rsqrt.21
  266.5 0.0 copy-done.2
  266.5 0.0 copy-done.3
  266.5 0.2 fusion.18
  266.7 0.0 copy-done.1
  266.7 0.8 fusion.8
  (6 shorter events, 0.1 us)
Async XLA Ops:
  0.0 4.2 %copy-start = (bf16[128,256]{1,0:T(8,128)(2,1)S(1)}, bf16[128,256]{1,0:T(8,128)(2,1)}, u32[]{:S(2)}) copy-start(bf16[128,256]{1,0:T(8,128)(2,1)} %param.15) | copy-start | bytes 196612
  16.4 197.2 %all-to-all-start.1 = ((bf16[16,2,16,32,128]{4,3,2,1,0:T(8,128)(2,1)}), bf16[16,2,16,32,128]{4,3,2,1,0:T(8,128)(2,1)}, u32[]{:S(2)}, u32[]{:S(2)}) async-start(bf16[16,2,16,32,128]{4,3,2,1,0:T(8,128)(2,1)} %stack.7), calls=%async_computation.1 | async-start | bytes 8388608 | tf_op jit(solution)/shard_map/all_to_all | solution.py:21
  235.7 14.2 %copy-start.4 = (bf16[128,128]{1,0:T(8,128)(2,1)S(1)}, bf16[128,128]{1,0:T(8,128)(2,1)}, u32[]{:S(2)}) copy-start(bf16[128,128]{1,0:T(8,128)(2,1)} %param.16) | copy-start | bytes 98308
  241.2 25.3 %copy-start.2 = (f32[128]{0:T(128)S(1)}, f32[128]{0:T(128)}, u32[]{:S(2)}) copy-start(f32[128]{0:T(128)} %param.18) | copy-start | bytes 1540
  241.2 25.3 %copy-start.3 = (f32[128]{0:T(128)S(1)}, f32[128]{0:T(128)}, u32[]{:S(2)}) copy-start(f32[128]{0:T(128)} %param.17) | copy-start | bytes 1540
  241.2 25.5 %copy-start.1 = (bf16[128,128]{1,0:T(8,128)(2,1)S(1)}, bf16[128,128]{1,0:T(8,128)(2,1)}, u32[]{:S(2)}) copy-start(bf16[128,128]{1,0:T(8,128)(2,1)} %param.19) | copy-start | bytes 98308
  242.8 23.0 %all-to-all-start.3 = ((bf16[8,16,32,128]{3,2,1,0:T(8,128)(2,1)}), bf16[8,16,32,128]{3,2,1,0:T(8,128)(2,1)S(1)}, u32[]{:S(2)}, u32[]{:S(2)}) async-start(bf16[8,16,32,128]{3,2,1,0:T(8,128)(2,1)} %reduce_sum.61), calls=%async_computation.3 | async-start | bytes 2097152 | tf_op jit(solution)/shard_map/all_to_all | solution.py:49
